TPU v7x, 32 devices: a whole 2x2x4 slice. The times are simulated.
32 devices in a mesh: section: 4 (over y, core), mp: 8 (over z, x).
Axes of the slice: x: 2, y: 2, z: 4, core: 2. Of those that a mesh axis runs over, the one named last changes fastest.
Arguments:
- arriving: bfloat16 [4, 768, 8192], P('section', None, 'mp'), may hold values from -6 to 6
- norm_gain: bfloat16 [4, 8192], P('section'), may hold values from 0.099609375 to 1.8984375
- w_query: bfloat16 [4, 2048, 8192], P('section', 'mp'), may hold values from -26 to 26
- w_key: bfloat16 [4, 1024, 8192], P('section', 'mp'), may hold values from -1 to 1
- w_value: bfloat16 [4, 1024, 8192], P('section', 'mp'), may hold values from -0.25 to 0.25
- w_out: bfloat16 [4, 2048, 8192], P('section', 'mp'), may hold values from -0.125 to 0.125
Outputs:
- attended: bfloat16 [4, 768, 8192], P('section', 'mp')
- stream_next: bfloat16 [4, 768, 8192], P('section', 'mp')
All inputs are finite; a program needn't handle non-finite values.
Results may differ from a plain program's by a relative error of at most 0.017.
Values may be sent and summed in bfloat16 or wider, within the bound.
A program may use at most 128 MiB of HBM per device.

v0:
```python
import math
import jax
import jax.numpy as jnp
from jax import lax
from jax.sharding import PartitionSpec as P

HD = 128
KV_HEADS = 8
rope_base = 500000.0
norm_eps = 1e-05


def shifted(block, axis, distance):
    devices = range(lax.axis_size(axis))
    route = [((i - distance) % len(devices), i) for i in devices]
    return lax.ppermute(block, axis, route)


def rotate_pairs(channel_major, pair_ids):
    channels = channel_major.shape[0]
    length = channel_major.shape[1]
    frequency = jnp.exp(pair_ids.astype(jnp.float32) * (-2.0 * math.log(rope_base) / HD))
    positions = jnp.arange(length, dtype=jnp.int32).astype(jnp.float32)
    angles = frequency[:, None] * positions[None, :]
    cos_table = jnp.cos(angles)
    sine_table = jnp.sin(angles)
    paired = channel_major.reshape(channels // 2, 2, length)
    even_part = paired[:, 0]
    odd_part = paired[:, 1]
    rotated = jnp.stack(
        [
            even_part * cos_table - odd_part * sine_table,
            even_part * sine_table + odd_part * cos_table,
        ],
        axis=1,
    )
    return rotated.reshape(channels, length)


def head_rows(table, kv_index):
    length = table.shape[1]
    grouped = table.reshape(HD // 2, KV_HEADS, 2, length)
    picked = lax.dynamic_slice_in_dim(grouped, kv_index, 1, 1)
    return picked.reshape(HD, length)


def normalize(hidden_in, gain_row):
    as_float = hidden_in.astype(jnp.float32)
    mean_square = jnp.mean(as_float * as_float, axis=1, keepdims=True)
    normed = (as_float * lax.rsqrt(mean_square + norm_eps) * gain_row).astype(jnp.bfloat16)
    return (as_float, normed)


def channel_product(weights, normed):
    return lax.dot_general(
        weights, normed, (((1,), (1,)), ((), ())), preferred_element_type=jnp.float32
    )


def local(arriving, norm_gain, w_query, w_key, w_value, w_out):
    local_block = arriving[0]
    gain_row = norm_gain[0].astype(jnp.float32)
    query_weights = w_query[0]
    key_weights = w_key[0]
    value_weights = w_value[0]
    out_weights = w_out[0]
    mp_count = lax.axis_size("mp")
    member = lax.axis_index("mp")
    length = local_block.shape[0]
    row_count = length // mp_count
    arrived = shifted(local_block, "section", 1)
    whole_rows = lax.all_gather(arrived, "mp", axis=1, tiled=True)
    full_float, normed_all = normalize(whole_rows, gain_row)
    residual = lax.dynamic_slice_in_dim(full_float, member * row_count, row_count, 0)
    projected = jnp.concatenate(
        [
            channel_product(query_weights, normed_all),
            channel_product(key_weights, normed_all),
            channel_product(value_weights, normed_all),
        ],
        axis=0,
    )
    q_width = query_weights.shape[0]
    k_width = key_weights.shape[0]
    query_pairs = jnp.arange(q_width // 2, dtype=jnp.int32) * 2 % HD // 2
    query_part = rotate_pairs(projected[:q_width], query_pairs).astype(jnp.bfloat16)
    key_pairs = (member * k_width + jnp.arange(k_width // 2, dtype=jnp.int32) * 2) // (2 * KV_HEADS)
    key_part = rotate_pairs(projected[q_width : q_width + k_width], key_pairs).astype(jnp.bfloat16)
    value_part = projected[q_width + k_width :].astype(jnp.bfloat16)
    key_all, value_all = (
        lax.all_gather(key_part, "mp", axis=0, tiled=True),
        lax.all_gather(value_part, "mp", axis=0, tiled=True),
    )
    local_heads = q_width // HD
    group_size = local_heads * mp_count // KV_HEADS
    kv_index = member * local_heads // group_size
    key_head = head_rows(key_all, kv_index)
    value_head = head_rows(value_all, kv_index)
    query_heads = query_part.reshape(local_heads, HD, length)
    score_scale = 1.0 / math.sqrt(HD)
    scores = (
        jnp.einsum("hdi,dj->hij", query_heads, key_head, preferred_element_type=jnp.float32)
        * score_scale
    )
    token_index = jnp.arange(length, dtype=jnp.int32)
    causal = token_index[:, None] >= token_index[None, :]
    scores = jnp.where(causal[None], scores, -1e30)
    row_max = jnp.max(scores, axis=-1, keepdims=True)
    exponent = jnp.exp(scores - row_max)
    row_total = jnp.sum(exponent, axis=-1, keepdims=True)
    weights = (exponent / row_total).astype(jnp.bfloat16)
    context = jnp.einsum(
        "hij,dj->ihd", weights, value_head, preferred_element_type=jnp.float32
    ).astype(jnp.bfloat16)
    context = context.reshape(length, q_width)
    full_term = jnp.dot(context, out_weights, preferred_element_type=jnp.float32)
    summed = lax.psum_scatter(
        full_term.astype(jnp.bfloat16), "mp", scatter_dimension=0, tiled=True
    ).astype(jnp.float32)
    attended = summed.astype(jnp.bfloat16)[None]
    stream_next = (residual + summed).astype(jnp.bfloat16)[None]
    return (attended, stream_next)


def solution(mesh):
    return jax.shard_map(
        local,
        mesh=mesh,
        in_specs=(
            P("section", None, "mp"),
            P("section", None),
            P("section", "mp", None),
            P("section", "mp", None),
            P("section", "mp", None),
            P("section", "mp", None),
        ),
        out_specs=(P("section", "mp", None), P("section", "mp", None)),
        check_vma=False,
    )
```

profile of v0, /device:TPU:0, one launch (start us, length us, event | category | flops | bytes accessed | tf_op | source)
XLA Modules:
  0.0 552.7 jit_solution(1898910907793692140)
XLA Ops:
  7.2 0.0 copy-start
  7.2 0.0 all-gather.4.cloned.1.call-start
  7.2 0.5 collective-permute-start
  7.8 20.4 %collective-permute-done = bf16[768,1024]{1,0:T(8,128)(2,1)} collective-permute-done((bf16[768,1024]{1,0:T(8,128)(2,1)}, bf16[768,1024]{1,0:T(8,128)(2,1)}, u32[]{:S(2)}, u32[]{:S(2)}) %collective-permute-start) | collective-permute-done | bytes 1572896 | tf_op jit(solution)/shard_map/ppermute | solution.py:16
  28.1 0.0 all-gather.4.cloned.1.call-update
  28.2 0.0 all-gather.6.cloned.1.call-start
  28.2 0.8 mul.223
  29.0 177.4 %all-gather.4.cloned.1.call-done = bf16[768,8192]{1,0:T(8,128)(2,1)} async-done(((bf16[768,1024]{1,0:T(8,128)(2,1)}), bf16[768,8192]{1,0:T(8,128)(2,1)}) %all-gather.4.cloned.1.call-update) | async-done | bytes 12582928 | tf_op jit(solution)/shard_map/all_gather | solution.py:72
  206.4 7.1 %multiply_reduce_fusion = f32[768]{0:T(1024)S(1)} fusion(bf16[768,8192]{1,0:T(8,128)(2,1)} %all-gather.4.cloned.1.call-done), kind=kLoop, calls=%fused_computation.2 | loop fusion | flops 18873600 | bytes 12585984 | tf_op jit(solution)/shard_map/reduce_sum | solution.py:49
  213.5 7.5 %multiply_convert_fusion = bf16[768,8192]{1,0:T(8,128)(2,1)S(1)} fusion(f32[8192]{0:T(1024)S(1)} %bitcast.56, f32[768]{0:T(1024)S(1)} %add_rsqrt_fusion, bf16[768,8192]{1,0:T(8,128)(2,1)} %all-gather.4.cloned.1.call-done), kind=kLoop, calls=%fused_computation.1 | loop fusion | flops 25165824 | bytes 25201664 | tf_op jit(solution)/shard_map/convert_element_type | solution.py:50
  221.0 0.0 copy-start.2
  221.0 4.5 copy-done.2
  225.5 0.0 copy-done
  225.5 4.1 fusion.24
  229.6 0.0 all-gather.6.cloned.1.call-update
  229.7 0.0 all-gather.8.cloned.1.call-start
  229.7 9.4 %fusion.18 = f32[128,768]{1,0:T(8,128)S(1)} fusion(bf16[768,8192]{1,0:T(8,128)(2,1)} %copy-done.2, bf16[1,128,8192]{2,1,0:T(8,128)(2,1)} %param.9), kind=kOutput, calls=%fused_computation.24 | convolution fusion | flops 1610612736 | bytes 15073280 | tf_op jit(solution)/shard_map/dot_general | solution.py:55
  239.2 0.2 reshape.284
  239.4 0.3 fusion.56
  239.8 0.8 fusion.42
  240.6 0.2 copy.22
  240.8 0.8 convert_element_type.92
  241.6 0.0 all-gather.8.cloned.1.call-update
  241.6 0.0 reduce-scatter.2.cloned.1.call-start
  241.7 0.2 iota_compare_fusion
  241.9 14.1 %fusion.14 = f32[256,768]{1,0:T(8,128)S(1)} fusion(bf16[768,8192]{1,0:T(8,128)(2,1)} %copy-done.2, bf16[1,256,8192]{2,1,0:T(8,128)(2,1)} %param.8), kind=kOutput, calls=%fused_computation.22 | convolution fusion | flops 3221225472 | bytes 17563648 | tf_op jit(solution)/shard_map/dot_general | solution.py:55
  255.9 0.5 reshape.283
  256.4 0.6 fusion.55
  257.0 1.7 fusion.34
  258.7 0.4 copy.19
  259.1 0.1 convert_element_type.90
  259.3 13.1 %all-gather.6.cloned.1.call-done = bf16[1024,768]{0,1:T(8,128)(2,1)} async-done(((bf16[128,768]{0,1:T(8,128)(2,1)}), bf16[1024,768]{0,1:T(8,128)(2,1)}) %all-gather.6.cloned.1.call-update) | async-done | bytes 1572880 | tf_op jit(solution)/shard_map/all_gather | solution.py:92
  272.4 1.7 copy.16
  274.1 1.5 reshape.281
  275.6 42.1 %all-gather.8.cloned.1.call-done = bf16[1024,768]{1,0:T(8,128)(2,1)} async-done(((bf16[128,768]{1,0:T(8,128)(2,1)}), bf16[1024,768]{1,0:T(8,128)(2,1)}) %all-gather.8.cloned.1.call-update) | async-done | bytes 1572880 | tf_op jit(solution)/shard_map/all_gather | solution.py:91
  317.7 3.5 reshape.285
  321.2 1.2 constant_dynamic-slice_fusion
  322.4 0.1 reshape.286
  322.5 0.1 reshape.290
  322.6 3.8 fusion.57
  326.4 3.0 fusion.17
  329.4 0.6 copy-done.3
  330.0 6.3 %convolution_convert_fusion = bf16[768,8192]{1,0:T(8,128)(2,1)} fusion(bf16[768,256]{0,1:T(8,128)(2,1)S(1)} %bitcast.55, bf16[1,256,8192]{2,1,0:T(8,128)(2,1)S(1)} %copy-done.3), kind=kOutput, calls=%fused_computation.3 | convolution fusion | flops 3227516928 | bytes 17170432 | tf_op jit(solution)/shard_map/dot_general | solution.py:116
  336.4 0.0 reduce-scatter.2.cloned.1.call-update
  336.4 0.0 copy-start.1
  336.4 14.5 %convert_element_type.84 = f32[768,8192]{1,0:T(8,128)} convert(bf16[768,8192]{1,0:T(8,128)(2,1)} %all-gather.4.cloned.1.call-done) | non-fusion elementwise | flops 6291456 | bytes 37748736 | tf_op jit(solution)/shard_map/convert_element_type | solution.py:48
  350.9 191.5 %reduce-scatter.2.cloned.1.call-done = bf16[96,8192]{1,0:T(8,128)(2,1)} async-done(((bf16[768,8192]{1,0:T(8,128)(2,1)}), bf16[96,8192]{1,0:T(8,128)(2,1)}) %reduce-scatter.2.cloned.1.call-update) | async-done | bytes 1572880 | tf_op jit(solution)/shard_map/reduce_scatter | solution.py:117
  542.4 3.8 fusion.13
  (8 shorter events, 0.1 us)
Async XLA Ops:
  7.2 218.4 %copy-start = (bf16[1,128,8192]{2,1,0:T(8,128)(2,1)S(1)}, bf16[1,128,8192]{2,1,0:T(8,128)(2,1)}, u32[]{:S(2)}) copy-start(bf16[1,128,8192]{2,1,0:T(8,128)(2,1)} %param.10) | copy-start | bytes 6291460
  7.2 199.3 %all-gather.4.cloned.1.call-start = ((), (), s32[]{:S(2)}) async-start(), calls=%async_computation.1 | async-start | bytes 14155776 | tf_op jit(solution)/shard_map/all_gather | solution.py:72
  7.2 20.9 %collective-permute-start = (bf16[768,1024]{1,0:T(8,128)(2,1)}, bf16[768,1024]{1,0:T(8,128)(2,1)}, u32[]{:S(2)}, u32[]{:S(2)}) collective-permute-start(bf16[768,1024]{1,0:T(8,128)(2,1)} %bitcast.57), channel_id=1, source_target_pairs={{24,0},{0,8},{8,16},{16,24},{25,1},{1,9},{9,17},{17,25},{26,2},{2,... | collective-permute-start | bytes 4718600 | tf_op jit(solution)/shard_map/ppermute | solution.py:16
  28.2 244.3 %all-gather.6.cloned.1.call-start = ((), (), s32[]{:S(2)}) async-start(), calls=%async_computation.2 | async-start | bytes 1769472 | tf_op jit(solution)/shard_map/all_gather | solution.py:92
  221.0 4.5 copy-start.2
  229.7 88.0 %all-gather.8.cloned.1.call-start = ((), (), s32[]{:S(2)}) async-start(), calls=%async_computation.3 | async-start | bytes 1769472 | tf_op jit(solution)/shard_map/all_gather | solution.py:91
  241.6 300.8 %reduce-scatter.2.cloned.1.call-start = ((), (), s32[]{:S(2)}) async-start(), calls=%async_computation.4 | async-start | bytes 14155776 | tf_op jit(solution)/shard_map/reduce_scatter | solution.py:117
  326.4 3.6 copy-start.3
  336.4 209.8 %copy-start.1 = (bf16[1,128,8192]{2,1,0:T(8,128)(2,1)S(1)}, bf16[1,128,8192]{2,1,0:T(8,128)(2,1)}, u32[]{:S(2)}) copy-start(bf16[1,128,8192]{2,1,0:T(8,128)(2,1)} %param.10) | copy-start | bytes 6291460
Sparse Core Ops, SparseCore 0:
  28.3 178.1 all-gather.3
  229.8 42.5 all-gather.5
  275.2 42.4 all-gather.7
  336.5 205.7 reduce-scatter.1
where the time goes:
time: 553 us
  waiting for transfers between devices  445 us (80%)
  matrix products  40.7 us (7%)
  other arithmetic  36.4 us (7%)
  local copies, waits for them, and re-layouts  16.4 us (3%)
  between operations  14 us (3%)
    reduce_scatter x1, waiting for transfers between devices, local(): lax.psum_scatter(full_term.astype(jnp.bfloat16), 'mp', scatter_dimension=...  191 us
    all_gather x1, waiting for transfers between devices, local(): whole_rows = lax.all_gather(arrived, 'mp', axis=1, tiled=True)  177 us
    all_gather x1, waiting for transfers between devices, local(): lax.all_gather(key_part, 'mp', axis=0, tiled=True)  42.1 us
    dot_general x3, matrix products, channel_product(): lax.dot_general(weights, normed, (((1,), (1,)), ((), ())), preferred_elem...  27.6 us
    ppermute x1, waiting for transfers between devices, shifted(): return lax.ppermute(block, axis, route)  20.4 us
    convert_element_type x1, other arithmetic, normalize(): as_float = hidden_in.astype(jnp.float32)  14.5 us
    all_gather x1, waiting for transfers between devices, local(): lax.all_gather(value_part, 'mp', axis=0, tiled=True)  13.1 us
  transfers between devices with their start and end apart: 5, of which 5 were waited for; matrix products, arithmetic and copies ran while one was open for 9% of the time, Pallas kernels for 0%

commit v1 on v0

--- a/solution.py
+++ b/solution.py
@@ -69,7 +69,7 @@
     length = local_block.shape[0]
     row_count = length // mp_count
     arrived = shifted(local_block, "section", 1)
-    whole_rows = lax.all_gather(arrived, "mp", axis=1, tiled=True)
+    whole_rows = jnp.concatenate(lax.all_gather(arrived, "mp"), axis=1)
     full_float, normed_all = normalize(whole_rows, gain_row)
     residual = lax.dynamic_slice_in_dim(full_float, member * row_count, row_count, 0)
     projected = jnp.concatenate(

time: 553 us -> 573 us (1.036)
  local copies, waits for them, and re-layouts: 16.4 us -> 36.8 us
    convert_element_type x2 -> x0, other arithmetic: 21.9 us -> none  [the longest x1 14.5 us: normalize(): as_float = hidden_in.astype(jnp.float32)]
    mul x0 -> x2, local copies, waits for them, and re-layouts: none -> 16.3 us  [normalize(): as_float * lax.rsqrt(mean_square + norm_eps) * gain_row]
    mul x1 -> x2, other arithmetic: 0.79 us -> 13 us  [normalize(): as_float * lax.rsqrt(mean_square + norm_eps) * gain_row]
    convert_element_type x0 -> x1, local copies, waits for them, and re-layouts: none -> 8.65 us  [normalize(): as_float = hidden_in.astype(jnp.float32)]
    unnamed x0 -> x1, other arithmetic: none -> 7.76 us
    all_gather x1, waiting for transfers between devices: 13.1 us -> 20.7 us  [local(): lax.all_gather(value_part, 'mp', axis=0, tiled=True)]
  transfers between devices with their start and end apart: 5 -> 5, of which waited for: 5 -> 5; matrix products, arithmetic and copies ran while one was open for 9% -> 7% of each run, Pallas kernels for 0% -> 0%
where the time goes in v1:
time: 573 us; the launch traced here: 572 us
  waiting for transfers between devices  450 us (79%)
  local copies, waits for them, and re-layouts  36.8 us (6%)
  matrix products  36.3 us (6%)
  other arithmetic  34.4 us (6%)
  between operations  14 us (2%)
    reduce_scatter x1, waiting for transfers between devices, local(): lax.psum_scatter(full_term.astype(jnp.bfloat16), 'mp', scatter_dimension=...  190 us
    all_gather x1, waiting for transfers between devices, local(): whole_rows = jnp.concatenate(lax.all_gather(arrived, 'mp'), axis=1)  177 us
    all_gather x1, waiting for transfers between devices, local(): lax.all_gather(key_part, 'mp', axis=0, tiled=True)  41.9 us
    dot_general x3, matrix products, channel_product(): lax.dot_general(weights, normed, (((1,), (1,)), ((), ())), preferred_elem...  23.2 us
    all_gather x1, waiting for transfers between devices, local(): lax.all_gather(value_part, 'mp', axis=0, tiled=True)  20.7 us
    ppermute x1, waiting for transfers between devices, shifted(): return lax.ppermute(block, axis, route)  20.4 us
    mul x2, local copies, waits for them, and re-layouts, normalize(): as_float * lax.rsqrt(mean_square + norm_eps) * gain_row  16.3 us
    mul x2, other arithmetic, normalize(): as_float * lax.rsqrt(mean_square + norm_eps) * gain_row  13 us
  transfers between devices with their start and end apart: 5, of which 5 were waited for; matrix products, arithmetic and copies ran while one was open for 7% of the time, Pallas kernels for 0%

profile of v1, /device:TPU:0, one launch (start us, length us, event | category | flops | bytes accessed | tf_op | source)
XLA Modules:
  0.0 572.1 jit_solution(11664445280410154016)
XLA Ops:
  7.2 0.0 copy-start
  7.2 0.0 all-gather.9.cloned.1.call-start
  7.2 0.5 collective-permute-start
  7.8 20.4 %collective-permute-done = bf16[768,1024]{1,0:T(8,128)(2,1)} collective-permute-done((bf16[768,1024]{1,0:T(8,128)(2,1)}, bf16[768,1024]{1,0:T(8,128)(2,1)}, u32[]{:S(2)}, u32[]{:S(2)}) %collective-permute-start) | collective-permute-done | bytes 1572896 | tf_op jit(solution)/shard_map/ppermute | solution.py:16
  28.1 0.0 all-gather.9.cloned.1.call-update
  28.2 0.0 all-gather.5.cloned.1.call-start
  28.2 0.8 convert_reduce_fusion
  29.1 177.4 %all-gather.9.cloned.1.call-done = bf16[6144,1024]{1,0:T(8,128)(2,1)} async-done(((bf16[768,1024]{1,0:T(8,128)(2,1)}), bf16[6144,1024]{1,0:T(8,128)(2,1)}) %all-gather.9.cloned.1.call-update) | async-done | bytes 12582928 | tf_op jit(solution)/shard_map/all_gather | solution.py:72
  206.4 7.1 %fusion.1 = f32[768]{0:T(1024)S(1)} fusion(bf16[8,768,1024]{2,1,0:T(8,128)(2,1)} %bitcast.62), kind=kLoop, calls=%fused_computation.4 | loop fusion | flops 18873600 | bytes 12585984 | tf_op jit(solution)/shard_map/reduce_sum | solution.py:49
  213.5 12.2 %fusion.4 = bf16[768,8,1024]{2,0,1:T(8,128)(2,1)} fusion(bf16[8,768,1024]{2,1,0:T(8,128)(2,1)} %bitcast.63, f32[8,1024]{1,0:T(8,128)S(1)} %reshape.326, f32[768]{0:T(1024)S(1)} %add_rsqrt_fusion), kind=kLoop, calls=%fused_computation.8 | loop fusion | flops 25165824 | bytes 25201664 | tf_op jit(solution)/shard_map/mul | solution.py:50
  225.7 16.3 %copy.25 = bf16[768,8,1024]{0,2,1:T(8,128)(2,1)} copy(bf16[768,8,1024]{2,0,1:T(8,128)(2,1)} %fusion.4) | data formatting | bytes 25165824 | tf_op jit(solution)/shard_map/mul | solution.py:50
  242.0 0.0 copy-done
  242.0 7.1 %fusion.28 = bf16[128,768]{0,1:T(8,128)(2,1)} fusion(bf16[768,8192]{0,1:T(8,128)(2,1)} %bitcast.65, bf16[1,128,8192]{2,1,0:T(8,128)(2,1)S(1)} %copy-done), kind=kOutput, calls=%fused_computation.31 | convolution fusion | flops 1610711040 | bytes 14876672 | tf_op jit(solution)/shard_map/dot_general | solution.py:55
  249.1 0.0 all-gather.5.cloned.1.call-update
  249.1 0.0 all-gather.7.cloned.1.call-start
  249.2 7.0 %fusion.22 = f32[128,768]{1,0:T(8,128)S(1)} fusion(bf16[768,8192]{0,1:T(8,128)(2,1)} %bitcast.66, bf16[1,128,8192]{2,1,0:T(8,128)(2,1)} %param.9), kind=kOutput, calls=%fused_computation.29 | convolution fusion | flops 1610612736 | bytes 15073280 | tf_op jit(solution)/shard_map/dot_general | solution.py:55
  256.2 0.2 reshape.322
  256.5 0.3 fusion.60
  256.8 0.8 fusion.46
  257.6 0.2 copy.32
  257.8 0.8 convert_element_type.108
  258.6 0.0 all-gather.7.cloned.1.call-update
  258.6 0.0 reduce-scatter.2.cloned.1.call-start
  258.7 0.2 iota_compare_fusion
  258.9 9.1 %fusion.18 = f32[256,768]{1,0:T(8,128)S(1)} fusion(bf16[768,8192]{0,1:T(8,128)(2,1)} %bitcast.67, bf16[1,256,8192]{2,1,0:T(8,128)(2,1)} %param.8), kind=kOutput, calls=%fused_computation.27 | convolution fusion | flops 3221225472 | bytes 17563648 | tf_op jit(solution)/shard_map/dot_general | solution.py:55
  267.9 0.5 reshape.321
  268.4 0.6 fusion.59
  269.0 1.7 fusion.38
  270.7 0.4 copy.29
  271.2 0.1 convert_element_type.106
  271.3 20.7 %all-gather.5.cloned.1.call-done = bf16[1024,768]{0,1:T(8,128)(2,1)} async-done(((bf16[128,768]{0,1:T(8,128)(2,1)}), bf16[1024,768]{0,1:T(8,128)(2,1)}) %all-gather.5.cloned.1.call-update) | async-done | bytes 1572880 | tf_op jit(solution)/shard_map/all_gather | solution.py:92
  292.0 1.7 copy.26
  293.7 1.5 reshape.319
  295.2 41.9 %all-gather.7.cloned.1.call-done = bf16[1024,768]{1,0:T(8,128)(2,1)} async-done(((bf16[128,768]{1,0:T(8,128)(2,1)}), bf16[1024,768]{1,0:T(8,128)(2,1)}) %all-gather.7.cloned.1.call-update) | async-done | bytes 1572880 | tf_op jit(solution)/shard_map/all_gather | solution.py:91
  337.1 3.5 reshape.323
  340.7 1.2 constant_dynamic-slice_fusion
  341.9 0.1 reshape.324
  342.0 0.1 reshape.332
  342.1 3.8 fusion.61
  345.8 3.0 fusion.21
  348.8 0.6 copy-done.2
  349.4 6.4 %convolution_convert_fusion = bf16[768,8192]{1,0:T(8,128)(2,1)} fusion(bf16[768,256]{0,1:T(8,128)(2,1)S(1)} %bitcast.70, bf16[1,256,8192]{2,1,0:T(8,128)(2,1)S(1)} %copy-done.2), kind=kOutput, calls=%fused_computation.7 | convolution fusion | flops 3227516928 | bytes 17170432 | tf_op jit(solution)/shard_map/dot_general | solution.py:116
  355.8 0.0 reduce-scatter.2.cloned.1.call-update
  355.8 7.8 %convert_bitcast_fusion = f32[8,96,8,1024]{3,2,1,0:T(8,128)S(1)} fusion(bf16[8,768,1024]{2,1,0:T(8,128)(2,1)} %bitcast.64), kind=kLoop, calls=%fused_computation.1 | loop fusion | flops 6291456 | bytes 37748736
  363.6 0.0 copy-start.1
  363.6 8.6 %copy.43 = f32[8,96,8,1024]{3,2,0,1:T(8,128)} copy(f32[8,96,8,1024]{3,2,1,0:T(8,128)S(1)} %convert_bitcast_fusion) | data formatting | bytes 50331648 | tf_op jit(solution)/shard_map/convert_element_type | solution.py:48
  372.2 189.5 %reduce-scatter.2.cloned.1.call-done = bf16[96,8192]{1,0:T(8,128)(2,1)} async-done(((bf16[768,8192]{1,0:T(8,128)(2,1)}), bf16[96,8192]{1,0:T(8,128)(2,1)}) %reduce-scatter.2.cloned.1.call-update) | async-done | bytes 1572880 | tf_op jit(solution)/shard_map/reduce_scatter | solution.py:117
  561.8 3.8 fusion.17
  (9 shorter events, 0.1 us)
Async XLA Ops:
  7.2 234.8 %copy-start = (bf16[1,128,8192]{2,1,0:T(8,128)(2,1)S(1)}, bf16[1,128,8192]{2,1,0:T(8,128)(2,1)}, u32[]{:S(2)}) copy-start(bf16[1,128,8192]{2,1,0:T(8,128)(2,1)} %param.10) | copy-start | bytes 6291460
  7.2 199.3 %all-gather.9.cloned.1.call-start = ((), (), s32[]{:S(2)}) async-start(), calls=%async_computation.4 | async-start | bytes 14155776 | tf_op jit(solution)/shard_map/all_gather | solution.py:72
  7.2 20.9 %collective-permute-start = (bf16[768,1024]{1,0:T(8,128)(2,1)}, bf16[768,1024]{1,0:T(8,128)(2,1)}, u32[]{:S(2)}, u32[]{:S(2)}) collective-permute-start(bf16[768,1024]{1,0:T(8,128)(2,1)} %bitcast.71), channel_id=1, source_target_pairs={{24,0},{0,8},{8,16},{16,24},{25,1},{1,9},{9,17},{17,25},{26,2},{2,... | collective-permute-start | bytes 4718600 | tf_op jit(solution)/shard_map/ppermute | solution.py:16
  28.2 263.8 %all-gather.5.cloned.1.call-start = ((), (), s32[]{:S(2)}) async-start(), calls=%async_computation.1 | async-start | bytes 1769472 | tf_op jit(solution)/shard_map/all_gather | solution.py:92
  249.1 88.0 %all-gather.7.cloned.1.call-start = ((), (), s32[]{:S(2)}) async-start(), calls=%async_computation.2 | async-start | bytes 1769472 | tf_op jit(solution)/shard_map/all_gather | solution.py:91
  258.6 303.2 %reduce-scatter.2.cloned.1.call-start = ((), (), s32[]{:S(2)}) async-start(), calls=%async_computation.3 | async-start | bytes 14155776 | tf_op jit(solution)/shard_map/reduce_scatter | solution.py:117
  345.8 3.6 copy-start.2
  363.6 202.0 %copy-start.1 = (bf16[1,128,8192]{2,1,0:T(8,128)(2,1)S(1)}, bf16[1,128,8192]{2,1,0:T(8,128)(2,1)}, u32[]{:S(2)}) copy-start(bf16[1,128,8192]{2,1,0:T(8,128)(2,1)} %param.10) | copy-start | bytes 6291460
Sparse Core Ops, SparseCore 0:
  28.3 178.1 all-gather.8
  249.2 42.6 all-gather.4
  294.7 42.3 all-gather.6
  355.9 205.7 reduce-scatter.1
